TPU v7x, 512 devices: a whole 4x4x16 slice. The times are simulated.
512 devices in a mesh: sector: 16 (over y, x_hi, core), member: 32 (over x_lo, z).
Axes of the slice: x: 4 (x_hi: 2, x_lo: 2; x = x_hi * 2 + x_lo), y: 4, z: 16, core: 2. Of those that a mesh axis runs over, the one named last changes fastest.
Arguments:
- state: bfloat16 [64, 4096, 256], P('member', 'sector'), may hold values from -18 to 18
- window_mask: int32 [4096, 256], P('sector'), may hold values 0 or 1
- window_index: int32 [4096], replicated, may hold values from 0 to 31, never falling along the last dimension, each value on 1 to 256 neighbouring positions
- w_space_qkv: bfloat16 [256, 768], replicated, may hold values from -0.375 to 0.375
- w_space_out: bfloat16 [256, 256], replicated, may hold values from -0.375 to 0.375
- temp_space: float32 [8], replicated, may hold values from 0.5 to 64
- w_ens_qkv: bfloat16 [256, 768], replicated, may hold values from -0.375 to 0.375
- w_ens_out: bfloat16 [256, 256], replicated, may hold values from -0.375 to 0.375
- temp_ens: float32 [8], replicated, may hold values from 0.5 to 64
- w_in: bfloat16 [256, 1024], replicated, may hold values from -0.375 to 0.375
- w_out: bfloat16 [1024, 256], replicated, may hold values from -0.1875 to 0.1875
Outputs:
- out_state: bfloat16 [64, 4096, 256], P('member', 'sector')
Inputs may be any that keep to these rules, and one draw needn't show every extreme that they name: `window_index`: window numbers never fall along the patches; a window spans 1 to 256 patches.
All inputs are finite; a program needn't handle non-finite values. No bound on the sum of `window_mask` on one device may be relied on, other than what follows from the above.
Results may differ from a plain program's by a relative error of at most 0.015.
The roundings to bfloat16 on the way count: a program that leaves them out, or rounds other values in their place, can miss the bound.
Values may be sent and summed in bfloat16 or wider, within the bound.
A program may use at most 64 MiB of HBM per device.

v0:
```python
import math

import jax
import jax.numpy as jnp
from jax import lax
from jax.sharding import PartitionSpec as P


def padded_2(x, sides, width):
    for axis, dim in sides:
        size, length = (lax.axis_size(axis), x.shape[dim])
        up = [(i, (i + 1) % size) for i in range(size)]
        down = [(j, i) for i, j in up]
        last = lax.slice_in_dim(x, length - width, length, axis=dim)
        first = lax.slice_in_dim(x, 0, width, axis=dim)
        before = lax.ppermute(last, axis, up)
        after = lax.ppermute(first, axis, down)
        x = jnp.concatenate([before, x, after], axis=dim)
    return x


def rms_rows(values):
    squares = jnp.mean(values * values, axis=-1, keepdims=True)
    return values * lax.rsqrt(squares + 1e-06)


def head_norm(values, total_heads):
    shaped = values.reshape(values.shape[:-1] + (total_heads, values.shape[-1] // total_heads))
    squares = jnp.mean(shaped * shaped, axis=-1, keepdims=True)
    return (shaped * lax.rsqrt(squares + 0.1)).reshape(values.shape)


def skew_band(table, span_width):
    row_count, columns = table.shape
    padded = jnp.pad(table, ((0, 0), (0, span_width + 1 - columns)))
    return padded.reshape(-1)[: row_count * span_width].reshape(row_count, span_width)


def attend_window(queries, keys, values, query_window, key_window, mask_rows, logit_scale):
    span_width = keys.shape[1]
    banded = skew_band(mask_rows + 1, span_width)
    same_window = query_window[:, None] == key_window[None, :]
    allowed = (banded == 2) | (banded == 1) & same_window
    scores = jnp.einsum("mqhd,mkhd->mhqk", queries, keys, preferred_element_type=jnp.float32)
    scores = scores * logit_scale[None, :, None, None]
    scores = jnp.where(allowed[None, None], scores, -1e30)
    row_max = jnp.max(scores, axis=-1, keepdims=True)
    exponent = jnp.exp(scores - row_max)
    weights = (exponent / jnp.sum(exponent, axis=-1, keepdims=True)).astype(jnp.bfloat16)
    return jnp.einsum("mhqk,mkhd->mqhd", weights, values, preferred_element_type=jnp.float32)


def member_attention_step(
    row_tile_size, query_key_value_weight, output_projection_weight, sampling_heat, total_heads
):
    everyone, patch_count, features = row_tile_size.shape
    head_width = features // total_heads
    normed = rms_rows(row_tile_size.astype(jnp.float32)).astype(jnp.bfloat16)
    projected = jnp.dot(
        normed.reshape(-1, features), query_key_value_weight, preferred_element_type=jnp.float32
    )
    projected = projected.reshape(everyone, patch_count, 3 * features)
    shape_heads = (everyone, patch_count, total_heads, head_width)
    query_rows = (
        head_norm(projected[..., :features], total_heads).astype(jnp.bfloat16).reshape(shape_heads)
    )
    key_rows = (
        head_norm(projected[..., features : 2 * features], total_heads)
        .astype(jnp.bfloat16)
        .reshape(shape_heads)
    )
    value_rows = projected[..., 2 * features :].astype(jnp.bfloat16).reshape(shape_heads)
    logit_scale = sampling_heat / math.sqrt(head_width)
    scores = jnp.einsum("mphd,nphd->phmn", query_rows, key_rows, preferred_element_type=jnp.float32)
    scores = scores * logit_scale[None, :, None, None]
    row_max = jnp.max(scores, axis=-1, keepdims=True)
    exponent = jnp.exp(scores - row_max)
    weights = (exponent / jnp.sum(exponent, axis=-1, keepdims=True)).astype(jnp.bfloat16)
    mixed_heads = jnp.einsum(
        "phmn,nphd->mphd", weights, value_rows, preferred_element_type=jnp.float32
    )
    mixed_heads = mixed_heads.reshape(everyone * patch_count, features).astype(jnp.bfloat16)
    update = jnp.dot(
        mixed_heads, output_projection_weight, preferred_element_type=jnp.float32
    ).reshape(row_tile_size.shape)
    return (row_tile_size.astype(jnp.float32) + update).astype(jnp.bfloat16)


def feed_forward(row_tile_size, w_in, w_out):
    features = row_tile_size.shape[-1]
    normed = rms_rows(row_tile_size.astype(jnp.float32)).astype(jnp.bfloat16).reshape(-1, features)
    hidden = jax.nn.gelu(jnp.dot(normed, w_in, preferred_element_type=jnp.float32)).astype(
        jnp.bfloat16
    )
    update = jnp.dot(hidden, w_out, preferred_element_type=jnp.float32).reshape(row_tile_size.shape)
    return (row_tile_size.astype(jnp.float32) + update).astype(jnp.bfloat16)


def on_device(
    state,
    window_mask,
    window_index,
    w_space_qkv,
    w_space_out,
    temp_space,
    w_ens_qkv,
    w_ens_out,
    temp_ens,
    w_in,
    w_out,
):
    members, tokens, features = state.shape
    total_heads = temp_space.shape[0]
    head_width = features // total_heads
    radius = window_mask.shape[1] // 2
    block_rows = min(tokens, 256)
    cycle_length = window_index.shape[0]
    first_patch = lax.axis_index("sector") * tokens
    normed = rms_rows(state.astype(jnp.float32)).astype(jnp.bfloat16)
    projected = jnp.dot(
        normed.reshape(-1, features), w_space_qkv, preferred_element_type=jnp.float32
    )
    projected = projected.reshape(members, tokens, 3 * features)
    query_rows = head_norm(projected[..., :features], total_heads).astype(jnp.bfloat16)
    key_rows = head_norm(projected[..., features : 2 * features], total_heads).astype(jnp.bfloat16)
    value_rows = projected[..., 2 * features :].astype(jnp.bfloat16)
    stacked = jnp.stack([key_rows, value_rows])
    rimmed = padded_2(stacked, (("sector", 2),), radius)
    key_cycle = rimmed[0]
    value_cycle = rimmed[1]
    cycle_index = jnp.concatenate(
        [window_index[cycle_length - radius :], window_index, window_index[:radius]]
    )
    query_heads = query_rows.reshape(members, tokens, total_heads, head_width)
    key_heads = key_cycle.reshape(members, tokens + 2 * radius, total_heads, head_width)
    value_heads = value_cycle.reshape(members, tokens + 2 * radius, total_heads, head_width)
    logit_scale = temp_space / math.sqrt(head_width)

    def one_block(offset):
        query_window = lax.dynamic_slice_in_dim(window_index, first_patch + offset, block_rows, 0)
        key_window = lax.dynamic_slice_in_dim(
            cycle_index, first_patch + offset, block_rows + 2 * radius, 0
        )
        attended = attend_window(
            query_heads, key_heads, value_heads, query_window, key_window, window_mask, logit_scale
        )
        return attended.astype(jnp.bfloat16)

    offsets = jnp.arange(tokens // block_rows, dtype=jnp.int32) * block_rows
    outputs = lax.map(one_block, offsets)
    mixed_heads = jnp.moveaxis(outputs, 0, 1).reshape(members * tokens, features)
    update = jnp.dot(mixed_heads, w_space_out, preferred_element_type=jnp.float32).reshape(
        state.shape
    )
    state_b = (state.astype(jnp.float32) + update).astype(jnp.bfloat16)
    group_size = lax.axis_size("member")
    patch_share = tokens // group_size
    regrouped = state_b.reshape(members, group_size, patch_share, features)
    parcel = lax.all_to_all(regrouped, "member", split_axis=1, concat_axis=0, tiled=True)
    everyone = parcel.shape[0]
    patch_count = parcel.shape[2]
    row_tile_size = parcel.reshape(everyone, patch_count, features)
    result = member_attention_step(row_tile_size, w_ens_qkv, w_ens_out, temp_ens, total_heads)
    result = feed_forward(result, w_in, w_out)
    gathered = result.reshape(everyone, 1, patch_count, features)
    returned = lax.all_to_all(gathered, "member", split_axis=0, concat_axis=1, tiled=True)
    state_c = returned.reshape(members, tokens, features)
    return state_c


def solution(mesh):
    return jax.shard_map(
        on_device,
        mesh=mesh,
        in_specs=(
            P("member", "sector", None),
            P("sector", None),
            P(),
            P(),
            P(),
            P(),
            P(),
            P(),
            P(),
            P(),
            P(),
        ),
        out_specs=P("member", "sector", None),
        check_vma=False,
    )
```

profile of v0, /device:TPU:28, one launch (start us, length us, event | category | flops | bytes accessed | tf_op | source)
XLA Modules:
  0.0 122.0 jit_solution(3852824276411489988)
XLA Ops:
  0.0 1.2 fusion.33
  1.2 1.5 %fusion.38 = f32[2,256,768]{2,1,0:T(8,128)S(1)} fusion(bf16[256,768]{1,0:T(8,128)(2,1)} %param.14, bf16[2,256,256]{2,1,0:T(8,128)(2,1)} %param.11, f32[2,256]{1,0:T(2,128)S(1)} %add_rsqrt_fusion.5), kind=kOutput, calls=%fused_computation.73 | convolution fusion | flops 201719808 | bytes 2230272 | tf_op jit(solution)/shard_map/dot_general | solution.py:120
  2.7 1.1 slice_multiply_fusion.2
  3.8 1.2 %copy.111 = f32[2,256,256]{1,2,0:T(8,128)S(1)} copy(f32[2,256,256]{2,1,0:T(8,128)} %get-tuple-element.29) | data formatting | bytes 1048576 | tf_op jit(solution)/shard_map/mul | solution.py:29
  6.0 1.2 %copy.112 = f32[2,256,256]{2,1,0:T(8,128)S(1)} copy(f32[2,256,256]{1,2,0:T(8,128)} %bitcast.93) | data formatting | bytes 1048576 | tf_op jit(solution)/shard_map/mul | solution.py:30
  7.2 2.1 %copy.108 = f32[2,256,256]{1,2,0:T(8,128)} copy(f32[2,256,256]{2,1,0:T(8,128)} %get-tuple-element.40) | data formatting | bytes 1048576 | tf_op jit(solution)/shard_map/mul | solution.py:29
  9.3 1.1 bitcast_reduce_fusion.3
  11.2 2.1 %copy.109 = f32[2,256,256]{2,1,0:T(8,128)} copy(f32[2,256,256]{1,2,0:T(8,128)} %bitcast.94) | data formatting | bytes 1048576 | tf_op jit(solution)/shard_map/mul | solution.py:30
  13.3 1.2 multiply_convert_fusion.3
  14.5 1.9 %collective-permute-start.1 = (bf16[2,2,128,256]{3,2,1,0:T(8,128)(2,1)S(1)}, bf16[2,2,128,256]{3,2,1,0:T(8,128)(2,1)S(1)}, u32[]{:S(2)}, u32[]{:S(2)}) collective-permute-start(bf16[2,2,128,256]{3,2,1,0:T(8,128)(2,1)S(1)} %get-tuple-element.48), channel_id=1, source_target_pairs={{32,0},{64,32},{96,64},{128,96},{160,128},{192,160},{224,192},{256... | collective-permute-start | bytes 786440 | tf_op jit(solution)/shard_map/ppermute | solution.py:17
  16.5 2.4 %collective-permute-start = (bf16[2,2,128,256]{3,2,1,0:T(8,128)(2,1)S(1)}, bf16[2,2,128,256]{3,2,1,0:T(8,128)(2,1)}, u32[]{:S(2)}, u32[]{:S(2)}) collective-permute-start(bf16[2,2,128,256]{3,2,1,0:T(8,128)(2,1)S(1)} %get-tuple-element.47), channel_id=1, source_target_pairs={{0,32},{32,64},{64,96},{96,128},{128,160},{160,192},{192,224},{224... | collective-permute-start | bytes 786440 | tf_op jit(solution)/shard_map/ppermute | solution.py:16
  20.6 6.3 %collective-permute-done = bf16[2,2,128,256]{3,2,1,0:T(8,128)(2,1)} collective-permute-done((bf16[2,2,128,256]{3,2,1,0:T(8,128)(2,1)S(1)}, bf16[2,2,128,256]{3,2,1,0:T(8,128)(2,1)}, u32[]{:S(2)}, u32[]{:S(2)}) %collective-permute-start) | collective-permute-done | bytes 262176 | tf_op jit(solution)/shard_map/ppermute | solution.py:16
  28.4 5.2 %fusion.66 = (f32[2,8,256]{2,1,0:T(8,128)S(1)}, f32[2,8,256,512]{3,2,1,0:T(8,128)}) fusion(f32[8]{0:T(128)S(1)} %broadcast_multiply_fusion.1, pred[256,512]{1,0:T(8,128)(4,1)S(1)} %and_or_fusion, bf16[2,256,8,32]{1,3,2,0:T(8,128)(2,1)S(1)} %bitcast.103, bf16[2,512,8,32]{1,3,2,0:T(8,128)(2,1)S(1)} %bitcast.101), kind=kOutput, calls=%fused_computation.111 | convolution fusion | flops 142606848 | bytes 9322528 | tf_op jit(solution)/shard_map/while/body/eval_jaxpr/sub | solution.py:48
  33.6 4.9 %fusion.23 = bf16[2,8,32,256]{3,2,1,0:T(8,128)(2,1)S(1)} fusion(bf16[2,512,8,32]{1,3,2,0:T(8,128)(2,1)S(1)} %bitcast.100, f32[2,8,256,512]{3,2,1,0:T(8,128)} %get-tuple-element.52, f32[2,8,256]{2,1,0:T(8,128)S(1)} %get-tuple-element.51), kind=kOutput, calls=%fused_computation.33 | convolution fusion | flops 138543104 | bytes 9191424 | tf_op jit(solution)/shard_map/while/body/eval_jaxpr/mhqk,mkhd->mqhd/dot_general | solution.py:50
  39.5 16.3 %all-to-all-start = ((bf16[2,32,8,256]{3,2,0,1:T(8,128)(2,1)}), bf16[2,32,8,256]{3,2,0,1:T(8,128)(2,1)S(1)}, u32[]{:S(2)}, u32[]{:S(2)}) async-start(bf16[2,32,8,256]{3,2,0,1:T(8,128)(2,1)} %copy.116), calls=%async_computation | async-start | bytes 524288 | tf_op jit(solution)/shard_map/all_to_all | solution.py:159
  55.8 21.6 %all-to-all-done = bf16[2,32,8,256]{3,2,0,1:T(8,128)(2,1)S(1)} async-done(((bf16[2,32,8,256]{3,2,0,1:T(8,128)(2,1)}), bf16[2,32,8,256]{3,2,0,1:T(8,128)(2,1)S(1)}, u32[]{:S(2)}, u32[]{:S(2)}) %all-to-all-start) | async-done | bytes 262176 | tf_op jit(solution)/shard_map/all_to_all | solution.py:159
  80.4 1.4 %copy.123 = f32[64,8,256]{0,2,1:T(8,128)S(1)} copy(f32[64,8,256]{2,1,0:T(8,128)} %get-tuple-element.25) | data formatting | bytes 1048576 | tf_op jit(solution)/shard_map/mul | solution.py:29
  82.0 1.2 copy.124
  83.2 1.4 %copy.120 = f32[64,8,256]{0,2,1:T(8,128)S(1)} copy(f32[64,8,256]{2,1,0:T(8,128)} %get-tuple-element.26) | data formatting | bytes 1048576 | tf_op jit(solution)/shard_map/mul | solution.py:29
  84.9 1.1 copy.121
  86.0 1.3 %multiply_convert_fusion.1 = (bf16[64,8,256]{2,1,0:T(8,128)(2,1)S(1)}, bf16[64,8,256]{2,1,0:T(8,128)(2,1)S(1)}) fusion(f32[64,8,256]{2,1,0:T(8,128)} %copy.124, f32[64,8,768]{2,1,0:T(8,128)S(1)} %fusion.36, f32[64,8,256]{2,1,0:T(8,128)} %copy.121), kind=kLoop, calls=%fused_computation.59 | loop fusion | flops 524288 | bytes 2621440 | tf_op jit(solution)/shard_map/convert_element_type | solution.py:69
  88.0 2.3 %fusion.67 = (f32[8,8,64]{2,1,0:T(8,128)S(1)}, f32[8,8,64,64]{2,3,1,0:T(8,128)}) fusion(f32[8]{0:T(128)S(1)} %broadcast_multiply_fusion, bf16[64,8,8,32]{0,3,2,1:T(8,128)(2,1)S(1)} %bitcast.97, bf16[64,8,8,32]{0,3,2,1:T(8,128)(2,1)S(1)} %bitcast.98), kind=kOutput, calls=%fused_computation.112 | convolution fusion | flops 17563712 | bytes 1589280 | tf_op jit(solution)/shard_map/sub | solution.py:77
  90.3 2.0 %convolution_convert_fusion = bf16[8,8,32,64]{3,2,1,0:T(8,128)(2,1)S(1)} fusion(bf16[64,8,8,32]{0,3,2,1:T(8,128)(2,1)S(1)} %bitcast.96, f32[8,8,64,64]{2,3,1,0:T(8,128)} %get-tuple-element.54, f32[8,8,64]{2,1,0:T(8,128)S(1)} %get-tuple-element.53), kind=kOutput, calls=%fused_computation.24 | convolution fusion | flops 17432576 | bytes 1589248 | tf_op jit(solution)/shard_map/phmn,nphd->mphd/dot_general | solution.py:79
  94.3 26.9 %all_to_all.24 = bf16[64,1,8,256]{3,2,1,0:T(8,128)(2,1)S(1)} all-to-all(bf16[64,1,8,256]{3,2,1,0:T(8,128)(2,1)S(1)} %fusion.25), channel_id=1, replica_groups=mesh['sector'=16,'member'=32] {'member'}, dimensions={0} | all-to-all | bytes 524288 | tf_op jit(solution)/shard_map/all_to_all | solution.py:166
  (74 shorter events, 12.8 us)
Async XLA Ops:
  0.0 93.1 %copy-start = (bf16[1024,256]{1,0:T(8,128)(2,1)S(1)}, bf16[1024,256]{1,0:T(8,128)(2,1)}, u32[]{:S(2)}) copy-start(bf16[1024,256]{1,0:T(8,128)(2,1)} %param.21) | copy-start | bytes 1572868
  13.3 5.6 %copy-start.9 = (f32[8]{0:T(128)S(1)}, f32[8]{0:T(128)}, u32[]{:S(2)}) copy-start(f32[8]{0:T(128)} %param.16) | copy-start | bytes 100
  13.3 5.6 %copy-start.4 = (s32[256,256]{1,0:T(8,128)S(1)}, s32[256,256]{1,0:T(8,128)}, u32[]{:S(2)}) copy-start(s32[256,256]{1,0:T(8,128)} %param.12) | copy-start | bytes 786436
  14.5 5.2 %copy-start.7 = (s32[4096]{0:T(1024)S(1)}, s32[4096]{0:T(1024)}, u32[]{:S(2)}) copy-start(s32[4096]{0:T(1024)} %param.13) | copy-start | bytes 49156
  14.5 6.0 %collective-permute-start.1 = (bf16[2,2,128,256]{3,2,1,0:T(8,128)(2,1)S(1)}, bf16[2,2,128,256]{3,2,1,0:T(8,128)(2,1)S(1)}, u32[]{:S(2)}, u32[]{:S(2)}) collective-permute-start(bf16[2,2,128,256]{3,2,1,0:T(8,128)(2,1)S(1)} %get-tuple-element.48), channel_id=1, source_target_pairs={{32,0},{64,32},{96,64},{128,96},{160,128},{192,160},{224,192},{256... | collective-permute-start | bytes 786440 | tf_op jit(solution)/shard_map/ppermute | solution.py:17
  16.5 10.4 %collective-permute-start = (bf16[2,2,128,256]{3,2,1,0:T(8,128)(2,1)S(1)}, bf16[2,2,128,256]{3,2,1,0:T(8,128)(2,1)}, u32[]{:S(2)}, u32[]{:S(2)}) collective-permute-start(bf16[2,2,128,256]{3,2,1,0:T(8,128)(2,1)S(1)} %get-tuple-element.47), channel_id=1, source_target_pairs={{0,32},{32,64},{64,96},{96,128},{128,160},{160,192},{192,224},{224... | collective-permute-start | bytes 786440 | tf_op jit(solution)/shard_map/ppermute | solution.py:16
  33.6 4.9 %copy-start.1 = (bf16[2,256,256]{2,1,0:T(8,128)(2,1)S(1)}, bf16[2,256,256]{2,1,0:T(8,128)(2,1)}, u32[]{:S(2)}) copy-start(bf16[2,256,256]{2,1,0:T(8,128)(2,1)} %param.11) | copy-start | bytes 786436
  33.6 4.9 %copy-start.5 = (bf16[256,256]{1,0:T(8,128)(2,1)S(1)}, bf16[256,256]{1,0:T(8,128)(2,1)}, u32[]{:S(2)}) copy-start(bf16[256,256]{1,0:T(8,128)(2,1)} %param.15) | copy-start | bytes 393220
  33.6 22.2 %copy-start.10 = (f32[8]{0:T(128)S(1)}, f32[8]{0:T(128)}, u32[]{:S(2)}) copy-start(f32[8]{0:T(128)} %param.19) | copy-start | bytes 100
  38.4 39.4 %copy-start.3 = (bf16[256,768]{1,0:T(8,128)(2,1)S(1)}, bf16[256,768]{1,0:T(8,128)(2,1)}, u32[]{:S(2)}) copy-start(bf16[256,768]{1,0:T(8,128)(2,1)} %param.17) | copy-start | bytes 1179652
  39.5 38.0 %all-to-all-start = ((bf16[2,32,8,256]{3,2,0,1:T(8,128)(2,1)}), bf16[2,32,8,256]{3,2,0,1:T(8,128)(2,1)S(1)}, u32[]{:S(2)}, u32[]{:S(2)}) async-start(bf16[2,32,8,256]{3,2,0,1:T(8,128)(2,1)} %copy.116), calls=%async_computation | async-start | bytes 524288 | tf_op jit(solution)/shard_map/all_to_all | solution.py:159
  87.7 2.6 %copy-start.2 = (bf16[64,8,256]{0,2,1:T(8,128)(2,1)S(1)}, bf16[64,8,256]{0,2,1:T(8,128)(2,1)}, u32[]{:S(2)}) copy-start(bf16[64,8,256]{0,2,1:T(8,128)(2,1)} %copy.119) | copy-start | bytes 786436
  90.3 2.4 %copy-start.6 = (bf16[256,256]{1,0:T(8,128)(2,1)S(1)}, bf16[256,256]{1,0:T(8,128)(2,1)}, u32[]{:S(2)}) copy-start(bf16[256,256]{1,0:T(8,128)(2,1)} %param.18) | copy-start | bytes 393220
  92.3 1.0 copy-start.8
where the time goes:
time: 123 us; the launch traced here: 122 us
  waiting for transfers between devices  27.9 us (23%)
  blocking collectives  26.9 us (22%)
  starting transfers between devices  20.6 us (17%)
  local copies, waits for them, and re-layouts  19 us (15%)
  matrix products  17.8 us (14%)
  other arithmetic  9.29 us (8%)
    all_to_all x1, blocking collectives, on_device(): lax.all_to_all(gathered, 'member', split_axis=0, concat_axis=1, tiled=True)  26.9 us
    all_to_all x1, waiting for transfers between devices, on_device(): lax.all_to_all(regrouped, 'member', split_axis=1, concat_axis=0, tiled=True)  21.6 us
    all_to_all x1, starting transfers between devices, on_device(): lax.all_to_all(regrouped, 'member', split_axis=1, concat_axis=0, tiled=True)  16.3 us
    mul x8, local copies, waits for them, and re-layouts, head_norm(): return (shaped * lax.rsqrt(squares + 0.1)).reshape(values.shape)  7.4 us
    ppermute x1, waiting for transfers between devices, padded_2(): before = lax.ppermute(last, axis, up)  6.25 us
    mul x4, local copies, waits for them, and re-layouts, head_norm(): squares = jnp.mean(shaped * shaped, axis=-1, keepdims=True)  6.05 us
    sub x1, matrix products, attend_window(): exponent = jnp.exp(scores - row_max)  5.19 us
    dot_general x1, matrix products, attend_window(): jnp.einsum('mhqk,mkhd->mqhd', weights, values, preferred_element_type=jnp...  4.87 us
  transfers between devices with their start and end apart: 3, of which 2 were waited for; matrix products, arithmetic and copies ran while one was open for 1% of the time, Pallas kernels for 0%

commit v1 on v0

v1 whole, which is shorter than its diff:
```python
import math

import jax
import jax.numpy as jnp
from jax import lax
from jax.experimental import pallas as pl
from jax.experimental.pallas import tpu as pltpu
from jax.sharding import PartitionSpec as P

F32 = jnp.float32
BF16 = jnp.bfloat16
MESH = pl.DeviceIdType.MESH
NEG = -1e30
LOG2E = 1.4426950408889634

D = 256
HEAD = 32
MEM = 2
TOK = 256
RAD = 128
CH = 2
QB = TOK // CH
KB = QB + 2 * RAD
NP = 32
NZ = 16
NS = 16
GH = 4
ROWS = NP * 8


def rms_rows(x):
    squares = jnp.sum(x * x, axis=-1, keepdims=True) * (1.0 / D)
    return x * lax.rsqrt(squares + 1e-06)


def head_norm(u, ones):
    sq = u * u
    hi = sq.astype(BF16)
    lo = (sq - hi.astype(F32)).astype(BF16)
    total = jnp.dot(hi, ones, preferred_element_type=F32) + jnp.dot(
        lo, ones, preferred_element_type=F32
    )
    return u * lax.rsqrt(total * (1.0 / HEAD) + 0.1)


def attend(q, k, v, bias, scale, ssc, psc, mxs):
    n, nk = q.shape[0], k.shape[0]
    lane = lax.broadcasted_iota(jnp.int32, (n, 128), 1) // HEAD
    halves = []
    for g in range(2):
        qg = q[:, g * 128 : (g + 1) * 128].astype(F32)
        kg = k[:, g * 128 : (g + 1) * 128]
        vg = v[:, g * 128 : (g + 1) * 128]
        stack = jnp.concatenate(
            [jnp.where(lane == h, qg, 0.0).astype(BF16) for h in range(GH)], axis=0
        )
        ssc[g, : GH * n, :nk] = lax.dot_general(
            stack, kg, (((1,), (1,)), ((), ())), preferred_element_type=F32
        )
        for h in range(GH):
            rows = slice(h * n, (h + 1) * n)
            s = ssc[g, rows, :nk] * scale[g * GH + h] + bias[...]
            mxs[g, rows] = jnp.broadcast_to(jnp.max(s, axis=-1, keepdims=True), (n, 128))
        for h in range(GH):
            rows = slice(h * n, (h + 1) * n)
            top = mxs[g, rows]
            s = ssc[g, rows, :nk] * scale[g * GH + h] + bias[...]
            e = jnp.exp2(s - jnp.concatenate([top] * (nk // 128), axis=1))
            ssc[g, rows, :nk] = e
            mxs[g, rows] = jnp.broadcast_to(jnp.sum(e, axis=-1, keepdims=True), (n, 128))
        for h in range(GH):
            rows = slice(h * n, (h + 1) * n)
            inv = 1.0 / mxs[g, rows]
            w = ssc[g, rows, :nk] * jnp.concatenate([inv] * (nk // 128), axis=1)
            psc[g, rows, :nk] = w.astype(BF16)
        r = jnp.dot(psc[g, : GH * n, :nk], vg, preferred_element_type=F32)
        o = r[:n]
        for h in range(1, GH):
            o = jnp.where(lane == h, r[h * n : (h + 1) * n], o)
        halves.append(o)
    return jnp.concatenate(halves, axis=1)


def kernel(
    state_h, mask_h, wid_h, wsq_h, wso_h, ts_s, weq_h, weo_h, te_s, wi_h, wo_h,
    out_ref,
    st, mk, wid, wsq, wso, weq, weo, wi, wo,
    halo, qa, ka, va, bias_a, bias_b, ones_s, ssc, psc, mxs, fs, fr, rs, rr,
    load_sem, halo_ssem, halo_rsem, f_ssem, f_rsem, r_ssem, r_rsem, know,
):
    s = lax.axis_index("sector")
    m = lax.axis_index("member")
    xl = m // NZ
    z = lax.rem(m, NZ)

    loads = []
    for i, (a, b) in enumerate(
        [
            (wid_h, wid),
            (mask_h, mk),
            (state_h, st),
            (wsq_h, wsq),
            (wso_h, wso),
            (weq_h, weq),
            (weo_h, weo),
            (wi_h, wi),
            (wo_h, wo),
        ]
    ):
        copy = pltpu.make_async_copy(a, b, load_sem.at[i])
        copy.start()
        loads.append(copy)

    def at(dx, dz):
        return (s, lax.rem(xl + dx, 2) * NZ + lax.rem(z + dz + NZ, NZ))

    right = (lax.rem(s + 1, NS), m)
    left = (lax.rem(s + NS - 1, NS), m)
    barrier = pltpu.get_barrier_semaphore()
    for dev in (right, left, at(0, 1), at(0, -1), at(1, 1), at(1, -1)):
        pl.semaphore_signal(barrier, 1, device_id=dev, device_id_type=MESH)

    ri = lax.broadcasted_iota(jnp.int32, (D, D), 0)
    ci = lax.broadcasted_iota(jnp.int32, (D, D), 1)
    ones_s[...] = jnp.where(ri // HEAD == ci // HEAD, 1.0, 0.0).astype(BF16)
    bias_b[...] = jnp.where(lax.rem(ri, 4) == lax.rem(ci, 4), 0.0, NEG)

    loads[0].wait()
    loads[1].wait()
    for c in range(CH):
        table = jnp.concatenate(
            [
                (mk[c * QB : (c + 1) * QB, :] + 1).astype(F32),
                jnp.zeros((QB, KB - 2 * RAD), F32),
            ],
            axis=1,
        )
        row = lax.broadcasted_iota(jnp.int32, (QB, KB), 0)
        for b in range(7):
            table = jnp.where(
                lax.rem(row // (1 << b), 2) == 1, pltpu.roll(table, 1 << b, 1), table
            )
        mine = jnp.broadcast_to(wid[pl.ds(2 * s + c, 1), :].astype(F32), (QB, 128)).T
        for t in range(KB // 128):
            theirs = wid[pl.ds(lax.rem(2 * s + 31 + c + t, 32), 1), :].astype(F32)
            part = table[:, t * 128 : (t + 1) * 128]
            ok = (part > 1.5) | ((part > 0.5) & (mine == jnp.broadcast_to(theirs, (QB, 128))))
            bias_a[c, :, t * 128 : (t + 1) * 128] = jnp.where(ok, 0.0, NEG)

    pl.semaphore_wait(barrier, 6)
    loads[2].wait()
    halos = []
    for i, dev in enumerate((right, left)):
        copy = pltpu.make_async_remote_copy(
            src_ref=st.at[:, pl.ds(RAD * (1 - i), RAD), :],
            dst_ref=halo.at[i],
            send_sem=halo_ssem.at[i],
            recv_sem=halo_rsem.at[i],
            device_id=dev,
            device_id_type=MESH,
        )
        copy.start()
        halos.append(copy)

    def tell(r):
        for dz in (1 << r, -(1 << r)):
            pl.semaphore_signal(know.at[r], 1, device_id=at(0, dz), device_id_type=MESH)

    tell(0)
    ones = ones_s[...]
    scale_a = [ts_s[h] * (LOG2E / math.sqrt(HEAD)) for h in range(8)]
    scale_b = [te_s[h] * (LOG2E / math.sqrt(HEAD)) for h in range(8)]

    loads[3].wait()
    for j in range(MEM):
        normed = rms_rows(st[j].astype(F32)).astype(BF16)
        proj = jnp.dot(normed, wsq[...], preferred_element_type=F32)
        qa[j] = head_norm(proj[:, :D], ones).astype(BF16)
        ka[j, RAD : RAD + TOK] = head_norm(proj[:, D : 2 * D], ones).astype(BF16)
        va[j, RAD : RAD + TOK] = proj[:, 2 * D :].astype(BF16)

    pl.semaphore_wait(know.at[0], 2)
    tell(1)

    def halo_keys(i):
        halos[i].wait_recv()
        rows = slice(0, RAD) if i == 0 else slice(RAD + TOK, RAD + TOK + RAD)
        for j in range(MEM):
            normed = rms_rows(halo[i, j].astype(F32)).astype(BF16)
            proj = jnp.dot(normed, wsq[:, D:], preferred_element_type=F32)
            ka[j, rows] = head_norm(proj[:, :D], ones).astype(BF16)
            va[j, rows] = proj[:, D:].astype(BF16)

    low = lax.rem(lax.broadcasted_iota(jnp.int32, (QB, D), 0), 8) < 4

    def window_chunk(c):
        after = []
        for j in range(MEM):
            q = qa[j, c * QB : (c + 1) * QB]
            keys = slice(c * QB, c * QB + KB)
            o = attend(q, ka[j, keys], va[j, keys], bias_a.at[c], scale_a, ssc, psc, mxs)
            upd = jnp.dot(o.astype(BF16), wso[...], preferred_element_type=F32)
            after.append(st[j, c * QB : (c + 1) * QB].astype(F32) + upd)
        even = jnp.where(low, after[0], pltpu.roll(after[1], 4, 0))
        odd = jnp.where(low, pltpu.roll(after[0], QB - 4, 0), after[1])
        fs[c, :, 0] = even.reshape(QB // 8, 8, D).astype(BF16)
        fs[c, :, 1] = odd.reshape(QB // 8, 8, D).astype(BF16)

    order = []
    for dz in (8, 7, -7, 6, -6, 5, -5, 4, -4, 3, -3, 2, -2, 1, -1, 0):
        for dx in (1, 0):
            if (dx, dz) != (0, 0):
                order.append((dx, dz))

    def slot(dx, dz):
        return dx * NZ + dz % NZ

    def forward(c):
        sends = []
        for dx, dz in order:
            dev = at(dx, dz)
            copy = pltpu.make_async_remote_copy(
                src_ref=fs.at[c, dev[1] // 2, lax.rem(dev[1], 2)],
                dst_ref=fr.at[c, slot(dx, dz)],
                send_sem=f_ssem.at[c],
                recv_sem=f_rsem.at[c],
                device_id=dev,
                device_id_type=MESH,
            )
            copy.start()
            sends.append(copy)
        fr[c, 0] = fs[c, m // 2, lax.rem(m, 2)]
        return sends

    def await_all(ref, sem):
        pltpu.make_async_copy(ref, ref, sem).wait()

    def member_chunk(c):
        await_all(fr.at[c, pl.ds(0, NP - 1)], f_rsem.at[c])
        x = fr[c].astype(F32).reshape(ROWS, D)
        normed = rms_rows(x).astype(BF16)
        proj = jnp.dot(normed, weq[...], preferred_element_type=F32)
        q = head_norm(proj[:, :D], ones).astype(BF16)
        k = head_norm(proj[:, D : 2 * D], ones).astype(BF16)
        v = proj[:, 2 * D :].astype(BF16)
        o = attend(q, k, v, bias_b, scale_b, ssc, psc, mxs)
        x = x + jnp.dot(o.astype(BF16), weo[...], preferred_element_type=F32)
        x = x.astype(BF16).astype(F32)
        normed = rms_rows(x).astype(BF16)
        hidden = jax.nn.gelu(jnp.dot(normed, wi[...], preferred_element_type=F32)).astype(BF16)
        x = x + jnp.dot(hidden, wo[...], preferred_element_type=F32)
        rs[c] = x.reshape(NP, 8, D).astype(BF16)

    def back(c):
        sends = []
        for dx, dz in order:
            copy = pltpu.make_async_remote_copy(
                src_ref=rs.at[c, slot(dx, -dz)],
                dst_ref=rr.at[c, m // 2, lax.rem(m, 2)],
                send_sem=r_ssem.at[c],
                recv_sem=r_rsem.at[c],
                device_id=at(dx, dz),
                device_id_type=MESH,
            )
            copy.start()
            sends.append(copy)
        rr[c, m // 2, lax.rem(m, 2)] = rs[c, 0]
        return sends

    halo_keys(0)
    pl.semaphore_wait(know.at[1], 2)
    tell(2)
    loads[4].wait()
    window_chunk(0)
    pl.semaphore_wait(know.at[2], 2)
    forward(0)
    halo_keys(1)
    window_chunk(1)
    forward(1)
    for i in range(5, 9):
        loads[i].wait()
    for c in range(CH):
        member_chunk(c)
        back(c)

    for c in range(CH):
        await_all(fr.at[c, pl.ds(0, NP - 1)], r_rsem.at[c])
        even = rr[c, :, 0].astype(F32).reshape(QB, D)
        odd = rr[c, :, 1].astype(F32).reshape(QB, D)
        rows = slice(c * QB, (c + 1) * QB)
        out_ref[0, rows] = jnp.where(low, even, pltpu.roll(odd, 4, 0)).astype(BF16)
        out_ref[1, rows] = jnp.where(low, pltpu.roll(even, QB - 4, 0), odd).astype(BF16)
    for c in range(CH):
        await_all(fr.at[c, pl.ds(0, NP - 1)], f_ssem.at[c])
        await_all(fr.at[c, pl.ds(0, NP - 1)], r_ssem.at[c])
    for copy in halos:
        copy.wait_send()


def on_device(
    state,
    window_mask,
    window_index,
    w_space_qkv,
    w_space_out,
    temp_space,
    w_ens_qkv,
    w_ens_out,
    temp_ens,
    w_in,
    w_out,
):
    hbm = pl.BlockSpec(memory_space=pl.ANY)
    smem = pl.BlockSpec(memory_space=pltpu.SMEM)
    return pl.pallas_call(
        kernel,
        out_shape=jax.ShapeDtypeStruct((MEM, TOK, D), BF16),
        in_specs=[hbm, hbm, hbm, hbm, hbm, smem, hbm, hbm, smem, hbm, hbm],
        out_specs=pl.BlockSpec(memory_space=pltpu.VMEM),
        scratch_shapes=[
            pltpu.VMEM((MEM, TOK, D), BF16),
            pltpu.VMEM((TOK, 2 * RAD), jnp.int32),
            pltpu.VMEM((32, 128), jnp.int32),
            pltpu.VMEM((D, 3 * D), BF16),
            pltpu.VMEM((D, D), BF16),
            pltpu.VMEM((D, 3 * D), BF16),
            pltpu.VMEM((D, D), BF16),
            pltpu.VMEM((D, 4 * D), BF16),
            pltpu.VMEM((4 * D, D), BF16),
            pltpu.VMEM((2, MEM, RAD, D), BF16),
            pltpu.VMEM((MEM, TOK, D), BF16),
            pltpu.VMEM((MEM, TOK + 2 * RAD, D), BF16),
            pltpu.VMEM((MEM, TOK + 2 * RAD, D), BF16),
            pltpu.VMEM((CH, QB, KB), F32),
            pltpu.VMEM((D, D), F32),
            pltpu.VMEM((D, D), BF16),
            pltpu.VMEM((2, GH * ROWS, KB), F32),
            pltpu.VMEM((2, GH * ROWS, KB), BF16),
            pltpu.VMEM((2, GH * ROWS, 128), F32),
            pltpu.VMEM((CH, NP // 2, 2, 8, D), BF16),
            pltpu.VMEM((CH, NP, 8, D), BF16),
            pltpu.VMEM((CH, NP, 8, D), BF16),
            pltpu.VMEM((CH, NP // 2, 2, 8, D), BF16),
            pltpu.SemaphoreType.DMA((9,)),
            pltpu.SemaphoreType.DMA((2,)),
            pltpu.SemaphoreType.DMA((2,)),
            pltpu.SemaphoreType.DMA((CH,)),
            pltpu.SemaphoreType.DMA((CH,)),
            pltpu.SemaphoreType.DMA((CH,)),
            pltpu.SemaphoreType.DMA((CH,)),
            pltpu.SemaphoreType.REGULAR((3,)),
        ],
        compiler_params=pltpu.CompilerParams(
            collective_id=0, has_side_effects=True, vmem_limit_bytes=48 * 1024 * 1024
        ),
        name="ensemble_block",
    )(
        state,
        window_mask,
        window_index.reshape(32, 128),
        w_space_qkv,
        w_space_out,
        temp_space,
        w_ens_qkv,
        w_ens_out,
        temp_ens,
        w_in,
        w_out,
    )


def solution(mesh):
    return jax.shard_map(
        on_device,
        mesh=mesh,
        in_specs=(P("member", "sector", None), P("sector", None)) + (P(),) * 9,
        out_specs=P("member", "sector", None),
        check_vma=False,
    )
```

time: 123 us -> 57.3 us (0.47)
  the two profiles are of different devices: /device:TPU:28 before, /device:TPU:24 now
where the time goes in v1:
time: 57.3 us; the launch traced here: 56.2 us
  Pallas kernels  46.3 us (81%)
  local copies, waits for them, and re-layouts  9.87 us (17%)
    pallas_call x1, Pallas kernels, on_device(): pl.pallas_call(kernel, out_shape=jax.ShapeDtypeStruct((MEM, TOK, D), BF16...  46.3 us
    unnamed x23, local copies, waits for them, and re-layouts  9.87 us

profile of v1, /device:TPU:24, one launch (start us, length us, event | category | flops | bytes accessed | tf_op | source)
XLA Modules:
  0.0 56.2 jit_solution(13464805540933108254)
XLA Ops:
  0.0 0.0 copy-start.10
  0.0 0.0 copy-start.9
  0.0 0.7 %copy-done.10 = f32[8]{0:T(128)S(1)} copy-done((f32[8]{0:T(128)S(1)}, f32[8]{0:T(128)}, u32[]{:S(2)}) %copy-start.10) | copy-done | bytes 56
  0.7 0.0 copy-done.9
  0.7 0.0 copy-start
  0.7 1.0 %copy-done = bf16[256,1024]{1,0:T(8,128)(2,1)S(1)} copy-done((bf16[256,1024]{1,0:T(8,128)(2,1)S(1)}, bf16[256,1024]{1,0:T(8,128)(2,1)}, u32[]{:S(2)}) %copy-start) | copy-done | bytes 524312
  1.7 0.0 copy-start.1
  1.7 1.0 %copy-done.1 = bf16[1024,256]{1,0:T(8,128)(2,1)S(1)} copy-done((bf16[1024,256]{1,0:T(8,128)(2,1)S(1)}, bf16[1024,256]{1,0:T(8,128)(2,1)}, u32[]{:S(2)}) %copy-start.1) | copy-done | bytes 524312
  2.8 0.0 copy-start.2
  2.8 1.0 %copy-done.2 = bf16[256,768]{1,0:T(8,128)(2,1)S(1)} copy-done((bf16[256,768]{1,0:T(8,128)(2,1)S(1)}, bf16[256,768]{1,0:T(8,128)(2,1)}, u32[]{:S(2)}) %copy-start.2) | copy-done | bytes 393240
  3.8 0.0 copy-start.3
  3.8 1.0 %copy-done.3 = bf16[256,768]{1,0:T(8,128)(2,1)S(1)} copy-done((bf16[256,768]{1,0:T(8,128)(2,1)S(1)}, bf16[256,768]{1,0:T(8,128)(2,1)}, u32[]{:S(2)}) %copy-start.3) | copy-done | bytes 393240
  4.7 0.0 copy-start.4
  4.8 0.9 %copy-done.4 = bf16[2,256,256]{2,1,0:T(8,128)(2,1)S(1)} copy-done((bf16[2,256,256]{2,1,0:T(8,128)(2,1)S(1)}, bf16[2,256,256]{2,1,0:T(8,128)(2,1)}, u32[]{:S(2)}) %copy-start.4) | copy-done | bytes 262168
  5.7 0.0 copy-start.5
  5.7 0.9 %copy-done.5 = s32[256,256]{1,0:T(8,128)S(1)} copy-done((s32[256,256]{1,0:T(8,128)S(1)}, s32[256,256]{1,0:T(8,128)}, u32[]{:S(2)}) %copy-start.5) | copy-done | bytes 262168
  6.7 0.0 copy-start.6
  6.7 0.9 %copy-done.6 = bf16[256,256]{1,0:T(8,128)(2,1)S(1)} copy-done((bf16[256,256]{1,0:T(8,128)(2,1)S(1)}, bf16[256,256]{1,0:T(8,128)(2,1)}, u32[]{:S(2)}) %copy-start.6) | copy-done | bytes 131096
  7.6 0.0 copy-start.7
  7.6 0.9 %copy-done.7 = bf16[256,256]{1,0:T(8,128)(2,1)S(1)} copy-done((bf16[256,256]{1,0:T(8,128)(2,1)S(1)}, bf16[256,256]{1,0:T(8,128)(2,1)}, u32[]{:S(2)}) %copy-start.7) | copy-done | bytes 131096
  8.5 0.0 copy-start.8
  8.5 0.7 %copy-done.8 = s32[4096]{0:T(1024)S(1)} copy-done((s32[4096]{0:T(1024)S(1)}, s32[4096]{0:T(1024)}, u32[]{:S(2)}) %copy-start.8) | copy-done | bytes 16408
  9.2 46.3 %ensemble_block.1 = bf16[2,256,256]{2,1,0:T(8,128)(2,1)S(1)} custom-call(bf16[2,256,256]{2,1,0:T(8,128)(2,1)S(1)} %copy-done.4, s32[256,256]{1,0:T(8,128)S(1)} %copy-done.5, s32[32,128]{1,0:T(8,128)S(1)} %bitcast.1, bf16[256,768]{1,0:T(8,128)(2,1)S(1)} %copy-done.2, bf16[256,256]{1,0:T(8,128)(2,1)S(1)} %copy-done.6, f32[8]{0:T(128)S(1)} %copy-done.9, ...), custom_call_target="tpu_custom_call" | custom-call | tf_op jit(solution)/shard_map/ensemble_block/pallas_call | solution.py:315
  55.5 0.7 %copy.13 = bf16[2,256,256]{2,1,0:T(8,128)(2,1)} copy(bf16[2,256,256]{2,1,0:T(8,128)(2,1)S(1)} %ensemble_block.1) | data formatting | bytes 524288
Async XLA Ops:
  0.0 0.7 %copy-start.10 = (f32[8]{0:T(128)S(1)}, f32[8]{0:T(128)}, u32[]{:S(2)}) copy-start(f32[8]{0:T(128)} %te_s.1) | copy-start | bytes 100
  0.0 0.7 %copy-start.9 = (f32[8]{0:T(128)S(1)}, f32[8]{0:T(128)}, u32[]{:S(2)}) copy-start(f32[8]{0:T(128)} %ts_s.1) | copy-start | bytes 100
  0.7 1.0 %copy-start = (bf16[256,1024]{1,0:T(8,128)(2,1)S(1)}, bf16[256,1024]{1,0:T(8,128)(2,1)}, u32[]{:S(2)}) copy-start(bf16[256,1024]{1,0:T(8,128)(2,1)} %wi_h.1) | copy-start | bytes 1572868
  1.7 1.0 %copy-start.1 = (bf16[1024,256]{1,0:T(8,128)(2,1)S(1)}, bf16[1024,256]{1,0:T(8,128)(2,1)}, u32[]{:S(2)}) copy-start(bf16[1024,256]{1,0:T(8,128)(2,1)} %wo_h.1) | copy-start | bytes 1572868
  2.8 1.0 %copy-start.2 = (bf16[256,768]{1,0:T(8,128)(2,1)S(1)}, bf16[256,768]{1,0:T(8,128)(2,1)}, u32[]{:S(2)}) copy-start(bf16[256,768]{1,0:T(8,128)(2,1)} %wsq_h.1) | copy-start | bytes 1179652
  3.8 1.0 %copy-start.3 = (bf16[256,768]{1,0:T(8,128)(2,1)S(1)}, bf16[256,768]{1,0:T(8,128)(2,1)}, u32[]{:S(2)}) copy-start(bf16[256,768]{1,0:T(8,128)(2,1)} %weq_h.1) | copy-start | bytes 1179652
  4.7 0.9 %copy-start.4 = (bf16[2,256,256]{2,1,0:T(8,128)(2,1)S(1)}, bf16[2,256,256]{2,1,0:T(8,128)(2,1)}, u32[]{:S(2)}) copy-start(bf16[2,256,256]{2,1,0:T(8,128)(2,1)} %state_h.1) | copy-start | bytes 786436
  5.7 0.9 %copy-start.5 = (s32[256,256]{1,0:T(8,128)S(1)}, s32[256,256]{1,0:T(8,128)}, u32[]{:S(2)}) copy-start(s32[256,256]{1,0:T(8,128)} %mask_h.1) | copy-start | bytes 786436
  6.7 0.9 %copy-start.6 = (bf16[256,256]{1,0:T(8,128)(2,1)S(1)}, bf16[256,256]{1,0:T(8,128)(2,1)}, u32[]{:S(2)}) copy-start(bf16[256,256]{1,0:T(8,128)(2,1)} %wso_h.1) | copy-start | bytes 393220
  7.6 0.9 %copy-start.7 = (bf16[256,256]{1,0:T(8,128)(2,1)S(1)}, bf16[256,256]{1,0:T(8,128)(2,1)}, u32[]{:S(2)}) copy-start(bf16[256,256]{1,0:T(8,128)(2,1)} %weo_h.1) | copy-start | bytes 393220
  8.5 0.7 %copy-start.8 = (s32[4096]{0:T(1024)S(1)}, s32[4096]{0:T(1024)}, u32[]{:S(2)}) copy-start(s32[4096]{0:T(1024)} %param.13) | copy-start | bytes 49156

commit v2 on v1

--- a/solution.py
+++ b/solution.py
@@ -25,6 +25,7 @@
 NZ = 16
 NS = 16
 GH = 4
+BACK = (0,1,2,3,4,15,5,14,6,13,7,12,8,11,9,10)
 ROWS = NP * 8
 
 
@@ -252,20 +253,25 @@
         rs[c] = x.reshape(NP, 8, D).astype(BF16)
 
     def back(c):
-        sends = []
-        for dx, dz in order:
-            copy = pltpu.make_async_remote_copy(
-                src_ref=rs.at[c, slot(dx, -dz)],
-                dst_ref=rr.at[c, m // 2, lax.rem(m, 2)],
-                send_sem=r_ssem.at[c],
-                recv_sem=r_rsem.at[c],
-                device_id=at(dx, dz),
-                device_id_type=MESH,
-            )
-            copy.start()
-            sends.append(copy)
+        for zd in BACK:
+            for dx in (1, 0):
+                there = lax.rem(xl + dx, 2) * NZ + zd
+
+                def send():
+                    pltpu.make_async_remote_copy(
+                        src_ref=rs.at[c, dx * NZ + lax.rem(z - zd + NZ, NZ)],
+                        dst_ref=rr.at[c, m // 2, lax.rem(m, 2)],
+                        send_sem=r_ssem.at[c],
+                        recv_sem=r_rsem.at[c],
+                        device_id=(s, there),
+                        device_id_type=MESH,
+                    ).start()
+
+                if dx == 1:
+                    send()
+                else:
+                    pl.when(zd != z)(send)
         rr[c, m // 2, lax.rem(m, 2)] = rs[c, 0]
-        return sends
 
     halo_keys(0)
     pl.semaphore_wait(know.at[1], 2)
@@ -351,7 +357,7 @@
             pltpu.SemaphoreType.REGULAR((3,)),
         ],
         compiler_params=pltpu.CompilerParams(
-            collective_id=0, has_side_effects=True, vmem_limit_bytes=48 * 1024 * 1024
+            collective_id=0, has_side_effects=True, vmem_limit_bytes=67043328
         ),
         name="ensemble_block",
     )(

time: 57.3 us -> 48.3 us (0.84); the launches traced: 56.2 us -> 48.1 us
  local copies, waits for them, and re-layouts: 9.87 us -> 1.67 us
    unnamed x23 -> x1, local copies, waits for them, and re-layouts: 9.87 us -> 1.67 us
where the time goes in v2:
time: 48.3 us; the launch traced here: 48.1 us
  Pallas kernels  46.4 us (96%)
  local copies, waits for them, and re-layouts  1.67 us (3%)
    pallas_call x1, Pallas kernels, on_device(): pl.pallas_call(kernel, out_shape=jax.ShapeDtypeStruct((MEM, TOK, D), BF16...  46.4 us
    unnamed x1, local copies, waits for them, and re-layouts  1.67 us

profile of v2, /device:TPU:24, one launch (start us, length us, event | category | flops | bytes accessed | tf_op | source)
XLA Modules:
  0.0 48.1 jit_solution(3630572290606518778)
XLA Ops:
  0.0 46.4 %ensemble_block.1 = bf16[2,256,256]{2,1,0:T(8,128)(2,1)} custom-call(bf16[2,256,256]{2,1,0:T(8,128)(2,1)} %state_h.1, s32[256,256]{1,0:T(8,128)} %mask_h.1, s32[32,128]{1,0:T(8,128)} %bitcast.1, bf16[256,768]{1,0:T(8,128)(2,1)} %wsq_h.1, bf16[256,256]{1,0:T(8,128)(2,1)} %wso_h.1, f32[8]{0:T(128)} %ts_s.1, bf16[256,768]{1,0:T(8,128)(2,1)} %weq_h.1, ...), custom_call_target="tpu_custom_call" | custom-call | tf_op jit(solution)/shard_map/ensemble_block/pallas_call | solution.py:321
  46.4 1.7 %copy.13 = bf16[2,256,256]{2,1,0:T(8,128)(2,1)} copy(bf16[2,256,256]{2,1,0:T(8,128)(2,1)} %ensemble_block.1) | data formatting | bytes 524288

commit v3 on v1

--- a/solution.py
+++ b/solution.py
@@ -25,6 +25,7 @@
 NZ = 16
 NS = 16
 GH = 4
+BACK = (0, 1, 2, 3, 8, 9, 10, 11, 7, 15, 6, 14, 5, 13, 4, 12)
 ROWS = NP * 8
 
 
@@ -82,9 +83,9 @@
 
 
 def kernel(
-    state_h, mask_h, wid_h, wsq_h, wso_h, ts_s, weq_h, weo_h, te_s, wi_h, wo_h,
+    state_h, mask_h, wid_h, wsq_h, wso_h, ts_h, weq_h, weo_h, te_h, wi_h, wo_h,
     out_ref,
-    st, mk, wid, wsq, wso, weq, weo, wi, wo,
+    st, mk, wid, wsq, wso, weq, weo, wi, wo, ts_s, te_s,
     halo, qa, ka, va, bias_a, bias_b, ones_s, ssc, psc, mxs, fs, fr, rs, rr,
     load_sem, halo_ssem, halo_rsem, f_ssem, f_rsem, r_ssem, r_rsem, know,
 ):
@@ -105,6 +106,8 @@
             (weo_h, weo),
             (wi_h, wi),
             (wo_h, wo),
+            (ts_h, ts_s),
+            (te_h, te_s),
         ]
     ):
         copy = pltpu.make_async_copy(a, b, load_sem.at[i])
@@ -168,6 +171,8 @@
 
     tell(0)
     ones = ones_s[...]
+    loads[9].wait()
+    loads[10].wait()
     scale_a = [ts_s[h] * (LOG2E / math.sqrt(HEAD)) for h in range(8)]
     scale_b = [te_s[h] * (LOG2E / math.sqrt(HEAD)) for h in range(8)]
 
@@ -252,20 +257,36 @@
         rs[c] = x.reshape(NP, 8, D).astype(BF16)
 
     def back(c):
-        sends = []
-        for dx, dz in order:
-            copy = pltpu.make_async_remote_copy(
-                src_ref=rs.at[c, slot(dx, -dz)],
-                dst_ref=rr.at[c, m // 2, lax.rem(m, 2)],
-                send_sem=r_ssem.at[c],
-                recv_sem=r_rsem.at[c],
-                device_id=at(dx, dz),
-                device_id_type=MESH,
-            )
-            copy.start()
-            sends.append(copy)
+        if c < CH - 1:
+            for dx, dz in order:
+                pltpu.make_async_remote_copy(
+                    src_ref=rs.at[c, slot(dx, -dz)],
+                    dst_ref=rr.at[c, m // 2, lax.rem(m, 2)],
+                    send_sem=r_ssem.at[c],
+                    recv_sem=r_rsem.at[c],
+                    device_id=at(dx, dz),
+                    device_id_type=MESH,
+                ).start()
+        else:
+            for zd in BACK:
+                for dx in (1, 0):
+                    there = lax.rem(xl + dx, 2) * NZ + zd
+
+                    def send():
+                        pltpu.make_async_remote_copy(
+                            src_ref=rs.at[c, dx * NZ + lax.rem(z - zd + NZ, NZ)],
+                            dst_ref=rr.at[c, m // 2, lax.rem(m, 2)],
+                            send_sem=r_ssem.at[c],
+                            recv_sem=r_rsem.at[c],
+                            device_id=(s, there),
+                            device_id_type=MESH,
+                        ).start()
+
+                    if dx == 1:
+                        send()
+                    else:
+                        pl.when(zd != z)(send)
         rr[c, m // 2, lax.rem(m, 2)] = rs[c, 0]
-        return sends
 
     halo_keys(0)
     pl.semaphore_wait(know.at[1], 2)
@@ -311,11 +332,10 @@
     w_out,
 ):
     hbm = pl.BlockSpec(memory_space=pl.ANY)
-    smem = pl.BlockSpec(memory_space=pltpu.SMEM)
     return pl.pallas_call(
         kernel,
         out_shape=jax.ShapeDtypeStruct((MEM, TOK, D), BF16),
-        in_specs=[hbm, hbm, hbm, hbm, hbm, smem, hbm, hbm, smem, hbm, hbm],
+        in_specs=[hbm] * 11,
         out_specs=pl.BlockSpec(memory_space=pltpu.VMEM),
         scratch_shapes=[
             pltpu.VMEM((MEM, TOK, D), BF16),
@@ -327,6 +347,8 @@
             pltpu.VMEM((D, D), BF16),
             pltpu.VMEM((D, 4 * D), BF16),
             pltpu.VMEM((4 * D, D), BF16),
+            pltpu.SMEM((8,), F32),
+            pltpu.SMEM((8,), F32),
             pltpu.VMEM((2, MEM, RAD, D), BF16),
             pltpu.VMEM((MEM, TOK, D), BF16),
             pltpu.VMEM((MEM, TOK + 2 * RAD, D), BF16),
@@ -341,7 +363,7 @@
             pltpu.VMEM((CH, NP, 8, D), BF16),
             pltpu.VMEM((CH, NP, 8, D), BF16),
             pltpu.VMEM((CH, NP // 2, 2, 8, D), BF16),
-            pltpu.SemaphoreType.DMA((9,)),
+            pltpu.SemaphoreType.DMA((11,)),
             pltpu.SemaphoreType.DMA((2,)),
             pltpu.SemaphoreType.DMA((2,)),
             pltpu.SemaphoreType.DMA((CH,)),
@@ -351,7 +373,7 @@
             pltpu.SemaphoreType.REGULAR((3,)),
         ],
         compiler_params=pltpu.CompilerParams(
-            collective_id=0, has_side_effects=True, vmem_limit_bytes=48 * 1024 * 1024
+            collective_id=0, has_side_effects=True, vmem_limit_bytes=67043328
         ),
         name="ensemble_block",
     )(

time: 57.3 us -> 47.8 us (0.83); the launches traced: 56.2 us -> 47.6 us
  local copies, waits for them, and re-layouts: 9.87 us -> 1.67 us
    unnamed x23 -> x1, local copies, waits for them, and re-layouts: 9.87 us -> 1.67 us
where the time goes in v3:
time: 47.8 us; the launch traced here: 47.6 us
  Pallas kernels  46 us (96%)
  local copies, waits for them, and re-layouts  1.67 us (3%)
    pallas_call x1, Pallas kernels, on_device(): pl.pallas_call(kernel, out_shape=jax.ShapeDtypeStruct((MEM, TOK, D), BF16...  46 us
    unnamed x1, local copies, waits for them, and re-layouts  1.67 us

profile of v3, /device:TPU:24, one launch (start us, length us, event | category | flops | bytes accessed | tf_op | source)
XLA Modules:
  0.0 47.6 jit_solution(130961921155372122)
XLA Ops:
  0.0 46.0 %ensemble_block.1 = bf16[2,256,256]{2,1,0:T(8,128)(2,1)} custom-call(bf16[2,256,256]{2,1,0:T(8,128)(2,1)} %state_h.1, s32[256,256]{1,0:T(8,128)} %mask_h.1, s32[32,128]{1,0:T(8,128)} %bitcast.1, bf16[256,768]{1,0:T(8,128)(2,1)} %wsq_h.1, bf16[256,256]{1,0:T(8,128)(2,1)} %wso_h.1, f32[8]{0:T(128)} %ts_h.1, bf16[256,768]{1,0:T(8,128)(2,1)} %weq_h.1, ...), custom_call_target="tpu_custom_call" | custom-call | tf_op jit(solution)/shard_map/ensemble_block/pallas_call | solution.py:335
  46.0 1.7 %copy.13 = bf16[2,256,256]{2,1,0:T(8,128)(2,1)} copy(bf16[2,256,256]{2,1,0:T(8,128)(2,1)} %ensemble_block.1) | data formatting | bytes 524288
